TPU v7x, 128 devices: a whole 4x4x4 slice. The times are simulated.
128 devices in a mesh: dp: 8 (over z, core), sp: 16 (over y, x).
Axes of the slice: x: 4, y: 4, z: 4, core: 2. Of those that a mesh axis runs over, the one named last changes fastest.
Arguments:
- queries_in: bfloat16 [16, 16384, 16, 128], P('dp', 'sp'), may hold values from -6 to 6
- keys_in: bfloat16 [16, 16384, 16, 128], P('dp', 'sp'), may hold values from -6 to 6
- values_in: bfloat16 [16, 16384, 16, 128], P('dp', 'sp'), may hold values from -6 to 6
- out_weight: bfloat16 [2048, 2048], P('dp'), may hold values from -0.125 to 0.125
Outputs:
- block_out: bfloat16 [16, 16384, 2048], P('dp', 'sp')
All inputs are finite; a program needn't handle non-finite values.
Results may differ from a plain program's by a relative error of at most 0.006.
Values may be sent and summed in bfloat16 or wider, within the bound.
A program may use at most 320 MiB of HBM per device.

v0:
```python
import jax
import jax.numpy as jnp
from jax import lax
from jax.sharding import PartitionSpec as P


def together(arrays, axis):
    ends = [0]
    for a in arrays:
        ends.append(ends[-1] + a.size)
    so_far = lax.psum(jnp.concatenate([a.ravel() for a in arrays]), axis)
    return tuple((so_far[b:e].reshape(a.shape) for a, b, e in zip(arrays, ends, ends[1:])))


def feature_map(values):
    wide = values.astype(jnp.float32)
    return (wide * wide + 0.1).astype(jnp.bfloat16)


def finish_heads(read, count):
    result = read * count**0.5
    return result.astype(jnp.bfloat16)


def look_up(features, state, mass):
    top = jnp.einsum(
        "bthd,bhde->bthe", features, state.astype(jnp.bfloat16), preferred_element_type=jnp.float32
    )
    bottom = jnp.einsum("bthd,bhd->bth", features.astype(jnp.float32), mass)
    return top / (bottom + 0.001)[..., None]


def on_device(queries_in, keys_in, values_in, out_weight):
    query_feature, key_feature = (feature_map(queries_in), feature_map(keys_in))
    count = queries_in.shape[1] * lax.axis_size("sp")
    part_state = jnp.einsum(
        "bthd,bthe->bhde", key_feature, values_in, preferred_element_type=jnp.float32
    )
    part_mass = jnp.sum(key_feature.astype(jnp.float32), axis=1)
    state, mass = together((part_state, part_mass), "sp")
    read = look_up(query_feature, state / count, mass / count)
    mixed = finish_heads(read, count)
    mixed = mixed.reshape(mixed.shape[0], mixed.shape[1], -1)
    return jnp.einsum(
        "btw,wv->btv",
        mixed,
        lax.all_gather(out_weight, "dp", axis=0, tiled=True),
        preferred_element_type=jnp.float32,
    ).astype(jnp.bfloat16)


def solution(mesh):
    placed = (
        P("dp", "sp", None, None),
        P("dp", "sp", None, None),
        P("dp", "sp", None, None),
        P("dp", None),
    )
    return jax.shard_map(
        on_device, mesh=mesh, in_specs=placed, out_specs=P("dp", "sp", None), check_vma=False
    )
```

profile of v0, /device:TPU:0, one launch (start us, length us, event | category | flops | bytes accessed | tf_op | source)
XLA Modules:
  0.0 168.0 jit_solution(11725410266001708717)
XLA Ops:
  7.4 0.0 all-reduce.2.cloned.1.call-start
  7.4 9.5 %add_convert_fusion.1 = (bf16[2,1024,16,128]{3,2,1,0:T(8,128)(2,1)}, f32[2,16,128]{2,1,0:T(8,128)S(1)}) fusion(bf16[2,1024,16,128]{3,2,1,0:T(8,128)(2,1)} %param.5), kind=kLoop, calls=%fused_computation.5 | loop fusion | flops 25161728 | bytes 16793600 | tf_op jit(solution)/shard_map/convert_element_type | solution.py:17
  16.8 13.9 %fusion.4 = f32[2,16,128,128]{3,2,1,0:T(8,128)S(1)} fusion(bf16[2,1024,16,128]{3,2,1,0:T(8,128)(2,1)} %param.6, bf16[2,1024,16,128]{3,2,1,0:T(8,128)(2,1)} %get-tuple-element.5), kind=kOutput, calls=%fused_computation.8 | convolution fusion | flops 1073741824 | bytes 18874368 | tf_op jit(solution)/shard_map/bthd,bthe->bhde/dot_general | solution.py:36
  30.8 1.4 pad_maximum_fusion
  32.2 0.0 all-reduce.2.cloned.1.call-update
  32.2 0.2 all-gather.2.cloned.1.call-start
  32.5 0.3 all-gather.2.cloned.1.call-update
  32.8 8.9 %add_convert_fusion = bf16[2,1024,16,128]{3,2,1,0:T(8,128)(2,1)} fusion(bf16[2,1024,16,128]{3,2,1,0:T(8,128)(2,1)} %param.4), kind=kLoop, calls=%fused_computation.3 | loop fusion | flops 16777216 | bytes 16777216 | tf_op jit(solution)/shard_map/convert_element_type | solution.py:17
  41.7 12.6 %copy.16 = bf16[2,1024,16,128]{1,3,2,0:T(8,128)(2,1)} copy(bf16[2,1024,16,128]{3,2,1,0:T(8,128)(2,1)} %add_convert_fusion) | data formatting | bytes 16777216 | tf_op jit(solution)/shard_map/convert_element_type | solution.py:17
  54.3 71.2 %all-reduce.2.cloned.1.call-done = f32[528384]{0:T(1024)} async-done(((f32[528384]{0:T(1024)}), f32[528384]{0:T(1024)}) %all-reduce.2.cloned.1.call-update) | async-done | bytes 2113552 | tf_op jit(solution)/shard_map/psum | solution.py:11
  125.5 0.0 copy-start.1
  125.5 0.9 slice_multiply_fusion.1
  126.4 0.0 copy-start
  126.4 4.7 %fusion.12 = f32[2,16,1,1024]{3,2,1,0:T(1,128)S(1)} fusion(f32[2,16,128,1]{2,3,1,0:T(1,128)S(1)} %bitcast.33, bf16[2,1024,16,128]{1,3,2,0:T(8,128)(2,1)} %copy.16), kind=kOutput, calls=%fused_computation.18 | convolution fusion | flops 8388608 | bytes 8536064 | tf_op jit(solution)/shard_map/bthd,bhd->bth/dot_general | solution.py:29
  131.1 0.0 copy-done.1
  131.1 0.1 fusion.10
  131.3 1.0 copy-done
  132.3 4.5 %fusion.1 = bf16[2,1024,16,128]{1,3,2,0:T(8,128)(2,1)} fusion(f32[2,1024,16]{1,2,0:T(8,128)S(1)} %fusion.11, bf16[2,16,128,128]{3,2,1,0:T(8,128)(2,1)S(1)} %bitcast.32, bf16[2,1024,16,128]{1,3,2,0:T(8,128)(2,1)S(1)} %copy-done), kind=kOutput, calls=%fused_computation.2 | convolution fusion | flops 1086324736 | bytes 17956864 | tf_op jit(solution)/shard_map/bthd,bhde->bthe/dot_general | solution.py:26
  136.8 0.0 all-gather.2.cloned.1.call-done
  136.8 23.7 %fusion.7 = bf16[2,1024,2048]{2,1,0:T(8,128)(2,1)} fusion(bf16[2,1024,2048]{1,2,0:T(8,128)(2,1)} %bitcast.35, bf16[2048,2048]{1,0:T(8,128)(2,1)} %all-gather.2.cloned.1.call-done), kind=kOutput, calls=%fused_computation.11 | convolution fusion | flops 17184063488 | bytes 25165824 | tf_op jit(solution)/shard_map/btw,wv->btv/dot_general | solution.py:44
  (1 shorter events, 0.0 us)
Async XLA Ops:
  7.4 118.1 %all-reduce.2.cloned.1.call-start = ((), (), s32[]{:S(2)}) async-start(), calls=%async_computation | async-start | bytes 4227072 | tf_op jit(solution)/shard_map/psum | solution.py:11
  32.2 104.6 %all-gather.2.cloned.1.call-start = ((), (), s32[]{:S(2)}) async-start(), calls=%async_computation.1 | async-start | bytes 9437184 | tf_op jit(solution)/shard_map/all_gather | solution.py:47
  125.5 5.6 %copy-start.1 = (f32[528384]{0:T(1024)S(1)}, f32[528384]{0:T(1024)}, u32[]{:S(2)}) copy-start(f32[528384]{0:T(1024)} %all-reduce.2.cloned.1.call-done) | copy-start | bytes 6340612
  126.4 5.9 %copy-start = (bf16[2,1024,16,128]{1,3,2,0:T(8,128)(2,1)S(1)}, bf16[2,1024,16,128]{1,3,2,0:T(8,128)(2,1)}, u32[]{:S(2)}) copy-start(bf16[2,1024,16,128]{1,3,2,0:T(8,128)(2,1)} %copy.16) | copy-start | bytes 25165828
Sparse Core Ops, SparseCore 0:
  32.3 93.1 all-reduce.1
Sparse Core Ops, SparseCore 1:
  34.4 52.2 all-gather.1
where the time goes:
time: 168 us
  waiting for transfers between devices  71.5 us (43%)
  matrix products  46.9 us (28%)
  other arithmetic  20.9 us (12%)
  between operations  14.9 us (9%)
  local copies, waits for them, and re-layouts  13.6 us (8%)
    psum x1, waiting for transfers between devices, together(): so_far = lax.psum(jnp.concatenate([a.ravel() for a in arrays]), axis)  71.2 us
    dot_general x1, matrix products, on_device(): jnp.einsum('btw,wv->btv', mixed, lax.all_gather(out_weight, 'dp', axis=0,...  23.7 us
    convert_element_type x2, other arithmetic, feature_map(): return (wide * wide + 0.1).astype(jnp.bfloat16)  18.4 us
    dot_general x1, matrix products, on_device(): jnp.einsum('bthd,bthe->bhde', key_feature, values_in, preferred_element_t...  13.9 us
    convert_element_type x1, local copies, waits for them, and re-layouts, feature_map(): return (wide * wide + 0.1).astype(jnp.bfloat16)  12.6 us
    dot_general x1, matrix products, look_up(): bottom = jnp.einsum('bthd,bhd->bth', features.astype(jnp.float32), mass)  4.72 us
    dot_general x1, matrix products, look_up(): jnp.einsum('bthd,bhde->bthe', features, state.astype(jnp.bfloat16), prefe...  4.55 us
  transfers between devices with their start and end apart: 2, of which 1 were waited for; matrix products, arithmetic and copies ran while one was open for 19% of the time, Pallas kernels for 0%

commit v1 on v0

--- a/solution.py
+++ b/solution.py
@@ -8,7 +8,7 @@
     ends = [0]
     for a in arrays:
         ends.append(ends[-1] + a.size)
-    so_far = lax.psum(jnp.concatenate([a.ravel() for a in arrays]), axis)
+    so_far = jnp.sum(lax.all_gather(jnp.concatenate([a.ravel() for a in arrays]), axis), axis=0)
     return tuple((so_far[b:e].reshape(a.shape) for a, b, e in zip(arrays, ends, ends[1:])))
 
 

time: 168 us -> 329 us (1.96)
  waiting for transfers between devices: 71.5 us -> 179 us
  local copies, waits for them, and re-layouts: 13.6 us -> 44.3 us
  other arithmetic: 20.9 us -> 44 us
    all_gather x0 -> x1, waiting for transfers between devices: none -> 179 us  [together(): lax.all_gather(jnp.concatenate([a.ravel() for a in arrays]), axis)]
    psum x1 -> x0, waiting for transfers between devices: 71.2 us -> none  [together(): so_far = lax.psum(jnp.concatenate([a.ravel() for a in arrays]), axis)]
    all_gather x0 -> x1, local copies, waits for them, and re-layouts: none -> 30.8 us  [together(): lax.all_gather(jnp.concatenate([a.ravel() for a in arrays]), axis)]
    reduce_sum x0 -> x1, other arithmetic: none -> 24 us  [together(): jnp.sum(lax.all_gather(jnp.concatenate([a.ravel() for a in arrays]), axis...]
  transfers between devices with their start and end apart: 2 -> 2, of which waited for: 1 -> 1; matrix products, arithmetic and copies ran while one was open for 19% -> 26% of each run, Pallas kernels for 0% -> 0%
where the time goes in v1:
time: 329 us; the launch traced here: 328 us
  waiting for transfers between devices  179 us (54%)
  matrix products  46.9 us (14%)
  local copies, waits for them, and re-layouts  44.3 us (13%)
  other arithmetic  44 us (13%)
  between operations  13.4 us (4%)
    all_gather x1, waiting for transfers between devices, together(): lax.all_gather(jnp.concatenate([a.ravel() for a in arrays]), axis)  179 us
    all_gather x1, local copies, waits for them, and re-layouts, together(): lax.all_gather(jnp.concatenate([a.ravel() for a in arrays]), axis)  30.8 us
    reduce_sum x1, other arithmetic, together(): jnp.sum(lax.all_gather(jnp.concatenate([a.ravel() for a in arrays]), axis...  24 us
    dot_general x1, matrix products, on_device(): jnp.einsum('btw,wv->btv', mixed, lax.all_gather(out_weight, 'dp', axis=0,...  23.7 us
    convert_element_type x2, other arithmetic, feature_map(): return (wide * wide + 0.1).astype(jnp.bfloat16)  18.4 us
    dot_general x1, matrix products, on_device(): jnp.einsum('bthd,bthe->bhde', key_feature, values_in, preferred_element_t...  13.9 us
    convert_element_type x1, local copies, waits for them, and re-layouts, feature_map(): return (wide * wide + 0.1).astype(jnp.bfloat16)  12.6 us
  transfers between devices with their start and end apart: 2, of which 1 were waited for; matrix products, arithmetic and copies ran while one was open for 26% of the time, Pallas kernels for 0%

profile of v1, /device:TPU:0, one launch (start us, length us, event | category | flops | bytes accessed | tf_op | source)
XLA Modules:
  0.0 328.0 jit_solution(7572258202788890514)
XLA Ops:
  6.5 0.0 all-gather.6.cloned.1.call-start
  6.5 9.5 %add_convert_fusion.1 = (bf16[2,1024,16,128]{3,2,1,0:T(8,128)(2,1)}, f32[2,16,128]{2,1,0:T(8,128)S(1)}) fusion(bf16[2,1024,16,128]{3,2,1,0:T(8,128)(2,1)} %param.5), kind=kLoop, calls=%fused_computation.5 | loop fusion | flops 25161728 | bytes 16793600 | tf_op jit(solution)/shard_map/convert_element_type | solution.py:17
  16.0 13.9 %fusion.4 = f32[2,16,128,128]{3,2,1,0:T(8,128)S(1)} fusion(bf16[2,1024,16,128]{3,2,1,0:T(8,128)(2,1)} %param.6, bf16[2,1024,16,128]{3,2,1,0:T(8,128)(2,1)} %get-tuple-element.5), kind=kOutput, calls=%fused_computation.8 | convolution fusion | flops 1073741824 | bytes 18874368 | tf_op jit(solution)/shard_map/bthd,bthe->bhde/dot_general | solution.py:36
  29.9 1.5 pad_maximum_fusion
  31.4 0.0 all-gather.6.cloned.1.call-update
  31.4 0.2 all-gather.4.cloned.1.call-start
  31.6 0.5 all-gather.4.cloned.1.call-update
  32.2 8.9 %add_convert_fusion = bf16[2,1024,16,128]{3,2,1,0:T(8,128)(2,1)} fusion(bf16[2,1024,16,128]{3,2,1,0:T(8,128)(2,1)} %param.4), kind=kLoop, calls=%fused_computation.3 | loop fusion | flops 16777216 | bytes 16777216 | tf_op jit(solution)/shard_map/convert_element_type | solution.py:17
  41.1 12.6 %copy.26 = bf16[2,1024,16,128]{1,3,2,0:T(8,128)(2,1)} copy(bf16[2,1024,16,128]{3,2,1,0:T(8,128)(2,1)} %add_convert_fusion) | data formatting | bytes 16777216 | tf_op jit(solution)/shard_map/convert_element_type | solution.py:17
  53.7 178.5 %all-gather.6.cloned.1.call-done = f32[8454144]{0:T(1024)} async-done(((f32[528384]{0:T(1024)}), f32[8454144]{0:T(1024)}) %all-gather.6.cloned.1.call-update) | async-done | bytes 33816592 | tf_op jit(solution)/shard_map/all_gather | solution.py:11
  232.2 30.8 %reshape.28 = f32[16,528384]{1,0:T(8,128)} reshape(f32[8454144]{0:T(1024)} %all-gather.6.cloned.1.call-done) | data formatting | bytes 67633152 | tf_op jit(solution)/shard_map/all_gather | solution.py:11
  263.0 24.0 %reduce_sum.19 = f32[528384]{0:T(1024)S(1)} reduce(f32[16,528384]{1,0:T(8,128)} %reshape.28, f32[]{:T(128)} %constant.2.clone.1), dimensions={0}, to_apply=%region_1.0 | reduce | flops 7925760 | bytes 35930116 | tf_op jit(solution)/shard_map/reduce_sum | solution.py:11
  287.1 0.0 copy-start
  287.1 4.7 %fusion.12 = f32[2,16,1,1024]{3,2,1,0:T(1,128)S(1)} fusion(f32[2,16,128,1]{2,3,1,0:T(1,128)S(1)} %bitcast.33, bf16[2,1024,16,128]{1,3,2,0:T(8,128)(2,1)} %copy.26), kind=kOutput, calls=%fused_computation.18 | convolution fusion | flops 8388608 | bytes 8536064 | tf_op jit(solution)/shard_map/bthd,bhd->bth/dot_general | solution.py:29
  291.9 0.1 fusion.10
  292.0 0.9 copy-done
  292.9 4.6 %fusion.1 = bf16[2,1024,16,128]{1,3,2,0:T(8,128)(2,1)} fusion(f32[2,1024,16]{1,2,0:T(8,128)S(1)} %fusion.11, bf16[2,16,128,128]{3,2,1,0:T(8,128)(2,1)S(1)} %bitcast.32, bf16[2,1024,16,128]{1,3,2,0:T(8,128)(2,1)S(1)} %copy-done), kind=kOutput, calls=%fused_computation.2 | convolution fusion | flops 1086324736 | bytes 17956864 | tf_op jit(solution)/shard_map/bthd,bhde->bthe/dot_general | solution.py:26
  297.4 0.0 all-gather.4.cloned.1.call-done
  297.4 23.7 %fusion.7 = bf16[2,1024,2048]{2,1,0:T(8,128)(2,1)} fusion(bf16[2,1024,2048]{1,2,0:T(8,128)(2,1)} %bitcast.35, bf16[2048,2048]{1,0:T(8,128)(2,1)} %all-gather.4.cloned.1.call-done), kind=kOutput, calls=%fused_computation.11 | convolution fusion | flops 17184063488 | bytes 25165824 | tf_op jit(solution)/shard_map/btw,wv->btv/dot_general | solution.py:44
  (2 shorter events, 0.0 us)
Async XLA Ops:
  6.5 225.7 %all-gather.6.cloned.1.call-start = ((), (), s32[]{:S(2)}) async-start(), calls=%async_computation.1 | async-start | bytes 35930112 | tf_op jit(solution)/shard_map/all_gather | solution.py:11
  31.4 266.0 %all-gather.4.cloned.1.call-start = ((), (), s32[]{:S(2)}) async-start(), calls=%async_computation | async-start | bytes 9437184 | tf_op jit(solution)/shard_map/all_gather | solution.py:47
  287.1 5.8 %copy-start = (bf16[2,1024,16,128]{1,3,2,0:T(8,128)(2,1)S(1)}, bf16[2,1024,16,128]{1,3,2,0:T(8,128)(2,1)}, u32[]{:S(2)}) copy-start(bf16[2,1024,16,128]{1,3,2,0:T(8,128)(2,1)} %copy.26) | copy-start | bytes 25165828
Sparse Core Ops, SparseCore 0:
  31.5 200.6 all-gather.5
  234.0 49.5 all-gather.3
